TPU v7x, 8 devices: a whole 2x2x1 slice. The times are simulated.
8 devices in a mesh: model: 2 (over z, y), data: 4 (over x, core).
Axes of the slice: x: 2, y: 2, z: 1, core: 2. Of those that a mesh axis runs over, the one named last changes fastest.
Arguments:
- act_in: bfloat16 [32768, 1024], P('data')
- grad_out: bfloat16 [32768, 1024], P('data')
- w_up: bfloat16 [2, 1024, 2816], P(None, None, 'model')
- w_down: bfloat16 [2, 2816, 1024], P(None, 'model')
- master_up: float32 [2, 1024, 2816], P(None, 'data', 'model')
- master_down: float32 [2, 2816, 1024], P(None, ('model', 'data'))
- mom_up: float32 [2, 1024, 2816], P(None, 'data', 'model')
- mom_down: float32 [2, 2816, 1024], P(None, ('model', 'data'))
- var_up: float32 [2, 1024, 2816], P(None, 'data', 'model')
- var_down: float32 [2, 2816, 1024], P(None, ('model', 'data'))
- learn_rate: float32 [1], replicated
- clip_norm: float32 [1], replicated
Outputs:
- output 1: bfloat16 [2, 1024, 2816], P(None, None, 'model')
- output 2: bfloat16 [2, 2816, 1024], P(None, 'model')
- output 3: float32 [2, 1024, 2816], P(None, 'data', 'model')
- output 4: float32 [2, 2816, 1024], P(None, ('model', 'data'))
- output 5: float32 [2, 1024, 2816], P(None, 'data', 'model')
- output 6: float32 [2, 2816, 1024], P(None, ('model', 'data'))
- output 7: float32 [2, 1024, 2816], P(None, 'data', 'model')
- output 8: float32 [2, 2816, 1024], P(None, ('model', 'data'))
- output 9: float32 [1], replicated
All inputs are finite; a program needn't handle non-finite values.
Results may differ from a plain program's by a relative error of at most 0.0014616.
Values are sent between devices in bfloat16 or wider.
A program may use at most 1 GiB of HBM per device.

v0:
```python
import jax
import jax.numpy as jnp
from jax import lax
from jax.sharding import PartitionSpec as P

STEP = 10
BETA_ONE = 0.9
BETA_TWO = 0.95
ADAM_EPS = 1e-8
NORM_EPS = 1e-6


def gelu_fwd(z_low):
    return jax.nn.gelu(z_low.astype(jnp.float32)).astype(jnp.bfloat16)


def gelu_back(z_low, grad_low):
    _, back_fn = jax.vjp(jax.nn.gelu, z_low.astype(jnp.float32))
    return back_fn(grad_low.astype(jnp.float32))[0].astype(jnp.bfloat16)


def adam_update(master_arr, mom_arr, var_arr, grad_arr, clip_scale, lr_val):
    scaled = clip_scale * grad_arr
    new_mom = BETA_ONE * mom_arr + (1.0 - BETA_ONE) * scaled
    new_var = BETA_TWO * var_arr + (1.0 - BETA_TWO) * scaled * scaled
    mom_hat = new_mom / (1.0 - BETA_ONE ** STEP)
    var_hat = new_var / (1.0 - BETA_TWO ** STEP)
    new_master = master_arr - lr_val * mom_hat / (jnp.sqrt(var_hat) + ADAM_EPS)
    return new_master, new_mom, new_var


def local_grads(act_in, grad_out, w_up, w_down):
    z_one = jnp.dot(act_in, w_up[0], preferred_element_type=jnp.float32).astype(jnp.bfloat16)
    act_one = gelu_fwd(z_one)
    hid_part = jnp.dot(act_one, w_down[0], preferred_element_type=jnp.float32)
    hid_two = lax.psum(hid_part, "model").astype(jnp.bfloat16)
    z_two = jnp.dot(hid_two, w_up[1], preferred_element_type=jnp.float32).astype(jnp.bfloat16)
    act_two = gelu_fwd(z_two)
    grad_w4 = jnp.einsum("bf,bd->fd", act_two, grad_out, preferred_element_type=jnp.float32)
    dact_two = jnp.einsum("bd,fd->bf", grad_out, w_down[1], preferred_element_type=jnp.float32).astype(jnp.bfloat16)
    dz_two = gelu_back(z_two, dact_two)
    grad_w3 = jnp.einsum("bd,bf->df", hid_two, dz_two, preferred_element_type=jnp.float32)
    dhid_part = jnp.einsum("bf,df->bd", dz_two, w_up[1], preferred_element_type=jnp.float32)
    dhid_two = lax.psum(dhid_part, "model").astype(jnp.bfloat16)
    grad_w2 = jnp.einsum("bf,bd->fd", act_one, dhid_two, preferred_element_type=jnp.float32)
    dact_one = jnp.einsum("bd,fd->bf", dhid_two, w_down[0], preferred_element_type=jnp.float32).astype(jnp.bfloat16)
    dz_one = gelu_back(z_one, dact_one)
    grad_w1 = jnp.einsum("bd,bf->df", act_in, dz_one, preferred_element_type=jnp.float32)
    return grad_w1, grad_w3, grad_w2, grad_w4


def solution(mesh):
    data_size = mesh.shape["data"]
    spec_rows = P("data", None)
    spec_wup = P(None, None, "model")
    spec_wdown = P(None, "model", None)
    spec_sup = P(None, "data", "model")
    spec_sdown = P(None, ("model", "data"), None)
    spec_scalar = P(None)

    def local_step(act_in, grad_out, w_up, w_down, master_up, master_down, mom_up, mom_down, var_up, var_down, learn_rate, clip_norm):
        grad_w1, grad_w3, grad_w2, grad_w4 = local_grads(act_in, grad_out, w_up, w_down)
        shard_w4 = lax.psum_scatter(grad_w4, "data", scatter_dimension=0, tiled=True)
        shard_w3 = lax.psum_scatter(grad_w3, "data", scatter_dimension=0, tiled=True)
        shard_w2 = lax.psum_scatter(grad_w2, "data", scatter_dimension=0, tiled=True)
        shard_w1 = lax.psum_scatter(grad_w1, "data", scatter_dimension=0, tiled=True)
        grad_up = jnp.stack([shard_w1, shard_w3]) / data_size
        grad_down = jnp.stack([shard_w2, shard_w4]) / data_size
        sq_local = jnp.sum(grad_up * grad_up) + jnp.sum(grad_down * grad_down)
        norm_val = jnp.sqrt(lax.psum(sq_local, ("model", "data")))
        clip_scale = jnp.minimum(1.0, clip_norm[0] / (norm_val + NORM_EPS))
        lr_val = learn_rate[0]
        new_master_up, new_mom_up, new_var_up = adam_update(master_up, mom_up, var_up, grad_up, clip_scale, lr_val)
        new_master_down, new_mom_down, new_var_down = adam_update(master_down, mom_down, var_down, grad_down, clip_scale, lr_val)
        new_w_up = lax.all_gather(new_master_up.astype(jnp.bfloat16), "data", axis=1, tiled=True)
        new_w_down = lax.all_gather(new_master_down.astype(jnp.bfloat16), "data", axis=1, tiled=True)
        return (new_w_up, new_w_down, new_master_up, new_master_down, new_mom_up, new_mom_down, new_var_up, new_var_down, norm_val.reshape(1))

    return jax.shard_map(local_step, mesh=mesh, in_specs=(spec_rows, spec_rows, spec_wup, spec_wdown, spec_sup, spec_sdown, spec_sup, spec_sdown, spec_sup, spec_sdown, spec_scalar, spec_scalar), out_specs=(spec_wup, spec_wdown, spec_sup, spec_sdown, spec_sup, spec_sdown, spec_sup, spec_sdown, spec_scalar), check_vma=False)
```

profile of v0, /device:TPU:0, one launch (start us, length us, event | category | flops | bytes accessed | tf_op | source)
XLA Modules:
  0.0 2122.9 jit_solution(3885899968851155359)
XLA Ops:
  7.2 33.4 %convolution_convert_fusion.2 = bf16[8192,1408]{1,0:T(8,128)(2,1)} fusion(bf16[8192,1024]{1,0:T(8,128)(2,1)} %param.12, bf16[2,1024,1408]{2,1,0:T(8,128)(2,1)} %param.14), kind=kOutput, calls=%fused_computation.36 | convolution fusion | flops 23633854464 | bytes 42729472 | tf_op jit(solution)/shard_map/dot_general | solution.py:33
  40.7 37.5 %fusion.36 = f32[8192,1024]{1,0:T(8,128)} fusion(bf16[2,1408,1024]{2,1,0:T(8,128)(2,1)S(1)} %copy-done.1, bf16[8192,1408]{1,0:T(8,128)(2,1)} %convolution_convert_fusion.2), kind=kOutput, calls=%fused_computation.56 | convolution fusion | flops 23737663488 | bytes 59506688 | tf_op jit(solution)/shard_map/dot_general | solution.py:35
  78.1 761.2 %all-reduce.2 = bf16[8192,1024]{1,0:T(8,128)(2,1)} all-reduce(f32[8192,1024]{1,0:T(8,128)} %fusion.36), channel_id=1, replica_groups=mesh['model'=2,'data'=4] {'model'}, use_global_device_ids=true, to_apply=%region_0.0 | all-reduce | flops 8388608 | bytes 50331648 | tf_op jit(solution)/shard_map/psum | solution.py:36
  839.3 33.4 %convolution_convert_fusion.1 = bf16[8192,1408]{1,0:T(8,128)(2,1)} fusion(bf16[8192,1024]{1,0:T(8,128)(2,1)} %all-reduce.2, bf16[2,1024,1408]{2,1,0:T(8,128)(2,1)} %param.14), kind=kOutput, calls=%fused_computation.35 | convolution fusion | flops 23633854464 | bytes 42729472 | tf_op jit(solution)/shard_map/dot_general | solution.py:37
  872.8 58.3 %fusion.4 = bf16[8192,1408]{1,0:T(8,128)(2,1)} fusion(bf16[8192,1408]{1,0:T(8,128)(2,1)} %convolution_convert_fusion.1, bf16[8192,1024]{1,0:T(8,128)(2,1)} %param.13, bf16[2,1408,1024]{2,1,0:T(8,128)(2,1)S(1)} %bitcast.59), kind=kOutput, calls=%fused_computation.16 | convolution fusion | flops 23887609856 | bytes 65798144 | tf_op jit(solution)/shard_map/bd,fd->bf/dot_general | solution.py:40
  931.1 31.8 %fusion.67 = f32[1024,1408]{0,1:T(8,128)} fusion(bf16[8192,1024]{1,0:T(8,128)(2,1)} %all-reduce.2, bf16[8192,1408]{1,0:T(8,128)(2,1)} %fusion.4), kind=kOutput, calls=%fused_computation.84 | convolution fusion | flops 23622320128 | bytes 45613056 | tf_op jit(solution)/shard_map/bd,bf->df/dot_general | solution.py:42
  962.9 33.4 %fusion.32 = f32[8192,1024]{1,0:T(8,128)} fusion(bf16[8192,1408]{1,0:T(8,128)(2,1)} %fusion.4, bf16[2,1024,1408]{2,1,0:T(8,128)(2,1)} %param.14), kind=kOutput, calls=%fused_computation.52 | convolution fusion | flops 23622320128 | bytes 59506688 | tf_op jit(solution)/shard_map/bf,df->bd/dot_general | solution.py:43
  996.3 753.4 %all-reduce.3 = bf16[8192,1024]{1,0:T(8,128)(2,1)} all-reduce(f32[8192,1024]{1,0:T(8,128)} %fusion.32), channel_id=1, replica_groups=mesh['model'=2,'data'=4] {'model'}, use_global_device_ids=true, to_apply=%region_1.0 | all-reduce | flops 8388608 | bytes 50331648 | tf_op jit(solution)/shard_map/psum | solution.py:44
  1749.7 58.8 %fusion.7.clone.4 = bf16[8192,1408]{1,0:T(8,128)(2,1)} fusion(bf16[8192,1408]{1,0:T(8,128)(2,1)} %convolution_convert_fusion.2, bf16[8192,1024]{1,0:T(8,128)(2,1)} %all-reduce.3, bf16[2,1408,1024]{2,1,0:T(8,128)(2,1)} %param.15), kind=kOutput, calls=%fused_computation.19.clone.clone.clone.1 | convolution fusion | flops 23887609856 | bytes 65798144 | tf_op jit(solution)/shard_map/bd,fd->bf/dot_general | solution.py:46
  1808.5 31.4 %convolution_bitcast_fusion = f32[1024,1408]{0,1:T(8,128)} fusion(bf16[8192,1024]{1,0:T(8,128)(2,1)} %param.12, bf16[8192,1408]{1,0:T(8,128)(2,1)} %fusion.7.clone.4), kind=kOutput, calls=%fused_computation.47 | convolution fusion | flops 23622320128 | bytes 45613056 | tf_op jit(solution)/shard_map/bd,bf->df/dot_general | solution.py:48
  1840.1 36.6 %fusion.22 = f32[1408,1024]{1,0:T(8,128)} fusion(bf16[8192,1024]{1,0:T(8,128)(2,1)} %param.13, bf16[8192,1408]{1,0:T(8,128)(2,1)} %convolution_convert_fusion.1), kind=kOutput, calls=%fused_computation.38 | convolution fusion | flops 23737663488 | bytes 45613056 | tf_op jit(solution)/shard_map/bf,bd->fd/dot_general | solution.py:39
  1876.7 36.9 %fusion.24 = f32[1408,1024]{1,0:T(8,128)} fusion(bf16[8192,1024]{1,0:T(8,128)(2,1)} %all-reduce.3, bf16[8192,1408]{1,0:T(8,128)(2,1)} %convolution_convert_fusion.2), kind=kOutput, calls=%fused_computation.39 | convolution fusion | flops 23737663488 | bytes 45613056 | tf_op jit(solution)/shard_map/bf,bd->fd/dot_general | solution.py:45
  1917.3 3.4 copy.21
  1927.2 11.3 reduce-scatter.11.cloned.1.call-done
  1938.5 50.4 %reduce-scatter.9.cloned.1.call-done = f32[352,1024]{1,0:T(8,128)} async-done(((f32[1408,1024]{1,0:T(8,128)}), f32[352,1024]{1,0:T(8,128)}) %reduce-scatter.9.cloned.1.call-update) | async-done | bytes 1441808 | tf_op jit(solution)/shard_map/reduce_scatter | solution.py:65
  1993.4 22.2 %psum.23 = f32[]{:T(128)} all-reduce(f32[]{:T(128)S(6)} %add.66), channel_id=1, replica_groups=mesh['model'=2,'data'=4] {'model','data'}, use_global_device_ids=true, to_apply=%region_8.0 | all-reduce | flops 1 | bytes 8 | tf_op jit(solution)/shard_map/psum | solution.py:70
  2016.4 7.1 fusion.65
  2023.6 8.1 fusion.63
  2031.7 3.4 copy.26
  2035.1 3.4 copy.27
  2040.7 26.2 %all-gather.3.cloned.1.call-done = bf16[2,1024,1408]{1,2,0:T(8,128)(2,1)} async-done(((bf16[2,256,1408]{1,2,0:T(8,128)(2,1)}), bf16[2,1024,1408]{1,2,0:T(8,128)(2,1)}) %all-gather.3.cloned.1.call-update) | async-done | bytes 5767184 | tf_op jit(solution)/shard_map/all_gather | solution.py:75
  2066.9 8.4 copy.25
  2075.3 33.6 %all-gather.5.cloned.1.call-done = bf16[2,1408,1024]{2,1,0:T(8,128)(2,1)} async-done(((bf16[2,352,1024]{2,1,0:T(8,128)(2,1)}), bf16[2,1408,1024]{2,1,0:T(8,128)(2,1)}) %all-gather.5.cloned.1.call-update) | async-done | bytes 5767184 | tf_op jit(solution)/shard_map/all_gather | solution.py:76
  2108.9 5.8 copy.37
  (28 shorter events, 14.5 us)
Async XLA Ops:
  7.2 1916.9 %reduce-scatter.7.cloned.1.call-start = ((), (), s32[]{:S(2)}) async-start(), calls=%async_computation.5 | async-start | bytes 7208960 | tf_op jit(solution)/shard_map/reduce_scatter | solution.py:64
  7.2 33.4 %copy-start.1 = (bf16[2,1408,1024]{2,1,0:T(8,128)(2,1)S(1)}, bf16[2,1408,1024]{2,1,0:T(8,128)(2,1)}, u32[]{:S(2)}) copy-start(bf16[2,1408,1024]{2,1,0:T(8,128)(2,1)} %param.15) | copy-start | bytes 17301508
  78.1 794.7 %slice-start = ((s8[5767168]{0:T(1024)(128)(4,1)}), s8[1572864]{0:T(1024)(128)(4,1)S(1)}, s32[]{:S(2)}) async-start(s8[5767168]{0:T(1024)(128)(4,1)} %bitcast.58), calls=%async_computation.10 | async-start | bytes 3145728
  839.3 33.4 %slice-start.1 = ((s8[5767168]{0:T(1024)(128)(4,1)}), s8[4194304]{0:T(1024)(128)(4,1)S(1)}, s32[]{:S(2)}) async-start(s8[5767168]{0:T(1024)(128)(4,1)} %bitcast.58), calls=%async_computation.11 | async-start | bytes 8388608
  962.9 961.2 %reduce-scatter.5.cloned.1.call-start = ((), (), s32[]{:S(2)}) async-start(), calls=%async_computation.4 | async-start | bytes 7208960 | tf_op jit(solution)/shard_map/reduce_scatter | solution.py:66
  1840.0 98.5 %reduce-scatter.11.cloned.1.call-start = ((), (), s32[]{:S(2)}) async-start(), calls=%async_computation.7 | async-start | bytes 7208960 | tf_op jit(solution)/shard_map/reduce_scatter | solution.py:63
  1876.7 112.3 %reduce-scatter.9.cloned.1.call-start = ((), (), s32[]{:S(2)}) async-start(), calls=%async_computation.6 | async-start | bytes 7208960 | tf_op jit(solution)/shard_map/reduce_scatter | solution.py:65
  1913.7 153.2 %all-gather.3.cloned.1.call-start = ((), (), s32[]{:S(2)}) async-start(), calls=%async_computation.8 | async-start | bytes 7208960 | tf_op jit(solution)/shard_map/all_gather | solution.py:75
  2023.5 14.9 copy-start
  2023.5 85.4 %all-gather.5.cloned.1.call-start = ((), (), s32[]{:S(2)}) async-start(), calls=%async_computation.9 | async-start | bytes 7208960 | tf_op jit(solution)/shard_map/all_gather | solution.py:76
Sparse Core Ops, SparseCore 0:
  963.0 48.4 reduce-scatter.6
  1840.1 47.7 reduce-scatter.4
  1890.5 48.0 reduce-scatter.10
  1940.9 48.0 reduce-scatter.8
  2023.7 43.2 all-gather.2
  2068.3 40.5 all-gather.4
where the time goes:
time: 2130 us; the launch traced here: 2120 us
  blocking collectives  1540 us (72%)
  matrix products  392 us (18%)
  waiting for transfers between devices  122 us (6%)
  local copies, waits for them, and re-layouts  32.2 us (2%)
  other arithmetic  21.5 us (1%)
    psum x1, blocking collectives, local_grads(): hid_two = lax.psum(hid_part, 'model').astype(jnp.bfloat16)  761 us
    psum x1, blocking collectives, local_grads(): dhid_two = lax.psum(dhid_part, 'model').astype(jnp.bfloat16)  753 us
    dot_general x1, matrix products, local_grads(): jnp.einsum('bd,fd->bf', dhid_two, w_down[0], preferred_element_type=jnp.f...  58.8 us
    dot_general x1, matrix products, local_grads(): jnp.einsum('bd,fd->bf', grad_out, w_down[1], preferred_element_type=jnp.f...  58.3 us
    reduce_scatter x1, waiting for transfers between devices, local_step(): lax.psum_scatter(grad_w2, 'data', scatter_dimension=0, tiled=True)  50.4 us
  transfers between devices with their start and end apart: 6, of which 4 were waited for; matrix products, arithmetic and copies ran while one was open for 11% of the time, Pallas kernels for 0%

commit v1 on v0

v1 whole, which is shorter than its diff:
```python
import functools

import jax
import jax.numpy as jnp
from jax import lax
from jax.experimental import pallas as pl
from jax.experimental.pallas import tpu as pltpu
from jax.sharding import PartitionSpec as P

STEP = 10
BETA_ONE = 0.9
BETA_TWO = 0.95
ADAM_EPS = 1e-8
NORM_EPS = 1e-6
GELU_A = 0.7978845608028654
GELU_B = GELU_A * 0.044715
BF16 = jnp.bfloat16
F32 = jnp.float32
DOT_NT = (((1,), (1,)), ((), ()))
DOT_TN = (((0,), (0,)), ((), ()))
VMEM_LIMIT = 60 * 2**20


def gelu(z):
    half = 0.5 * z
    return half + half * jnp.tanh(z * (z * z * GELU_B + GELU_A))


def gelu_grad(z):
    sq = z * z
    sig = 0.5 * jnp.tanh(z * (sq * GELU_B + GELU_A)) + 0.5
    return sig + z * (sq * (6.0 * GELU_B) + 2.0 * GELU_A) * (sig - sig * sig)


def gelu_both(z):
    sq = z * z
    sig = 0.5 * jnp.tanh(z * (sq * GELU_B + GELU_A)) + 0.5
    act = z * sig
    return act, sig + (act - act * sig) * (sq * (6.0 * GELU_B) + 2.0 * GELU_A)


def col_chunks(width, step):
    return [slice(lo, min(lo + step, width)) for lo in range(0, width, step)]


def forward_body(x_ref, dy_ref, w1_ref, w2_ref, w3_ref, w4_ref, z1_ref, h_ref, a3_ref, q3_ref, a1_scr):
    x = x_ref[...]
    for cols in col_chunks(w1_ref.shape[1], 256):
        z = jnp.dot(x, w1_ref[:, cols], preferred_element_type=F32).astype(BF16)
        z1_ref[:, cols] = z
        a1_scr[:, cols] = gelu(z.astype(F32)).astype(BF16)
    h = jnp.dot(a1_scr[...], w2_ref[...], preferred_element_type=F32).astype(BF16)
    h_ref[...] = h
    dy = dy_ref[...]
    for cols in col_chunks(w3_ref.shape[1], 256):
        z = jnp.dot(h, w3_ref[:, cols], preferred_element_type=F32).astype(BF16)
        e = lax.dot_general(dy, w4_ref[cols, :], DOT_NT, preferred_element_type=F32).astype(BF16)
        act, slope = gelu_both(z.astype(F32))
        a3_ref[:, cols] = act.astype(BF16)
        q3_ref[:, cols] = (e.astype(F32) * slope).astype(BF16)


def grad_body(left_ref, right_ref, out_ref, *, act):
    left = left_ref[...]
    if act:
        left = gelu(left.astype(F32)).astype(BF16)
    out_ref[...] = lax.dot_general(left, right_ref[...], DOT_TN, preferred_element_type=F32)


def resident(shape):
    return pl.BlockSpec(shape, lambda i: (0,) * len(shape), pipeline_mode=pl.Buffered(1))


def row_tile(rows, width):
    return pl.BlockSpec((rows, width), lambda i: (i, 0))


def params():
    return pltpu.CompilerParams(vmem_limit_bytes=VMEM_LIMIT)


def cost(flops, moved):
    return pl.CostEstimate(flops=flops, bytes_accessed=moved, transcendentals=0)


def forward(x, dy, w1, w2, w3, w4, tile=512):
    rows, d = x.shape
    f = w1.shape[1]
    wide, slim = jax.ShapeDtypeStruct((rows, f), BF16), jax.ShapeDtypeStruct((rows, d), BF16)
    return pl.pallas_call(
        forward_body,
        grid=(rows // tile,),
        in_specs=[row_tile(tile, d), row_tile(tile, d), resident((d, f)), resident((f, d)), resident((d, f)), resident((f, d))],
        out_specs=[row_tile(tile, f), row_tile(tile, d), row_tile(tile, f), row_tile(tile, f)],
        out_shape=[wide, slim, wide, wide],
        scratch_shapes=[pltpu.VMEM((tile, f), BF16)],
        compiler_params=params(),
        cost_estimate=cost(8 * rows * d * f, 6 * rows * f),
        name="forward",
    )(x, dy, w1, w2, w3, w4)


MESH = pl.DeviceIdType.MESH
TILE = 512
BLOCK = 256


class Lanes:
    def __init__(self):
        data = lax.axis_index("data")
        self.model = lax.axis_index("model")
        self.x, self.core = data // 2, data % 2
        self.mate = {"data": 2 * self.x + (1 - self.core)}
        self.over_x = {"data": 2 * (1 - self.x) + self.core}
        self.over_y = {"model": 1 - self.model}
        self.all = (self.mate, self.over_x, self.over_y)

    def shard(self, far, core):
        return 2 * ((self.x + far) % 2) + core


def greet(lanes):
    barrier = pltpu.get_barrier_semaphore()
    for peer in lanes.all:
        pl.semaphore_signal(barrier, inc=1, device_id=peer, device_id_type=MESH)
    pl.semaphore_wait(barrier, len(lanes.all))


class Reducer:
    def __init__(self, lanes, up, bufs, send, recv, scratch, local):
        self.lanes, self.up, self.send, self.recv, self.local = lanes, up, send, recv, local
        self.grad, self.mated, self.chip, self.from_y, self.from_x, self.part_a, self.part_b, self.last_x, self.last_y = bufs
        self.left, self.right, self.out = scratch
        self.rows = self.left.shape[0] // 2
        self.copies = {}

    def block(self, half, shard):
        if self.up:
            rows, width = 2 * self.rows, self.left.shape[1]
            return self.grad.at[pl.ds(shard * rows, rows), pl.ds(half * width, width)]
        rows = 2 * self.rows
        return self.grad.at[pl.ds(half * 4 * rows + shard * rows, rows), :]

    def remote(self, slot, src, dst, peer):
        copy = pltpu.make_async_remote_copy(src, dst, self.send.at[slot], self.recv.at[slot], device_id=peer, device_id_type=MESH)
        self.copies[slot] = copy
        return copy

    def mate_copies(self):
        lanes = self.lanes
        out = []
        for half in range(2):
            for far in range(2):
                shard = lanes.shard(far, 1 - lanes.core)
                out.append(self.remote(2 * half + far, self.block(half, shard), self.mated.at[half, far], lanes.mate))
        return out

    def first(self, half, far):
        lanes, rows = self.lanes, self.rows
        chip = self.chip.at[half, far]
        sends = []
        if half == 1:
            sends.append(self.remote(4 + far, chip.at[pl.ds(0, rows)], self.from_y.at[far], lanes.over_y))
        if far == 1:
            sends.append(self.remote(6 + half, chip.at[pl.ds(rows, rows)], self.from_x.at[half], lanes.over_x))
        return Job(self, self.block(half, lanes.shard(far, lanes.core)), self.mated.at[half, far], chip, 2 * rows, (2 * half + far,), sends)

    def second_a(self, far):
        dst = self.part_a.at[far]
        sends = [self.remote(8, dst, self.last_x, self.lanes.over_x)] if far == 1 else []
        return Job(self, self.chip.at[0, far].at[pl.ds(0, self.rows)], self.from_y.at[far], dst, self.rows, (4 + far,), sends)

    def second_b(self, half):
        dst = self.part_b.at[half]
        sends = [self.remote(9, dst, self.last_y, self.lanes.over_y)] if half == 1 else []
        return Job(self, self.chip.at[half, 0].at[pl.ds(self.rows, self.rows)], self.from_x.at[half], dst, self.rows, (6 + half,), sends)

    def firsts(self):
        return [self.first(1, 1), self.first(1, 0), self.first(0, 1), self.first(0, 0)]

    def seconds(self):
        return [self.second_a(1), self.second_b(1), self.second_a(0), self.second_b(0)]

    def finish(self):
        for slot in (8, 9):
            self.copies[slot].wait_recv()
        for slot in range(10):
            self.copies[slot].wait_send()


class Job:
    def __init__(self, owner, left, right, dst, rows, arrivals, sends):
        view = lambda ref: ref.at[pl.ds(0, rows)]
        self.owner, self.arrivals, self.sends = owner, arrivals, sends
        self.bufs = view(owner.left), view(owner.right), view(owner.out)
        self.loads = [pltpu.make_async_copy(src, buf, owner.local.at[k]) for k, (src, buf) in enumerate(zip((left, right), self.bufs))]
        self.store = pltpu.make_async_copy(self.bufs[2], dst, owner.local.at[2])

    def start(self):
        for slot in self.arrivals:
            self.owner.copies[slot].wait_recv()
        for load in self.loads:
            load.start()

    def add(self):
        for load in self.loads:
            load.wait()
        left, right, out = self.bufs
        out[...] = left[...] + right[...]
        self.store.start()

    def done(self):
        self.store.wait()
        for copy in self.sends:
            copy.start()


class Plan:
    def __init__(self):
        self.pending = None

    def arrange(self, jobs):
        chain = []
        for at in sorted(jobs):
            chain.append((at, self.pending, jobs[at]))
            self.pending = jobs[at]
        return chain

    @staticmethod
    def beside(step, chain, work):
        for at, old, job in chain:
            @pl.when(step == at)
            def _(old=old, job=job):
                if old is not None:
                    old.done()
                job.start()
        work()
        for at, old, job in chain:
            @pl.when(step == at)
            def _(job=job):
                job.add()

    def run(self, jobs):
        for job in jobs:
            if self.pending is not None:
                self.pending.done()
            job.start()
            job.add()
            self.pending = job

    def flush(self):
        if self.pending is not None:
            self.pending.done()
        self.pending = None


def reduce_kernel(a3, q3, z1, h, x, dy, w3, w2, *refs):
    outs, scratch = refs[:37], refs[37:]
    q1 = outs[0]
    bufs = [outs[1 + 9 * k:10 + 9 * k] for k in range(4)]
    res0, res1, w3_v, w2_v, up_l, up_r, up_o, dn_l, dn_r, dn_o, send, recv, local, fetch = scratch
    lanes = Lanes()
    greet(lanes)
    reds = [Reducer(lanes, up, bufs[k], send.at[k], recv.at[k], (up_l, up_r, up_o) if up else (dn_l, dn_r, dn_o), local)
            for k, up in enumerate((False, True, False, True))]
    down4, up3, down2, up1 = reds
    load = lambda src, dst, k: pltpu.make_async_copy(src, dst, fetch.at[k])
    get_dy, get_h, get_x, get_w3, get_w2 = load(dy, res0, 0), load(h, res1, 1), load(x, res1, 2), load(w3, w3_v, 3), load(w2, w2_v, 4)
    rows, d = x.shape
    f = a3.shape[1]
    plan = Plan()

    def down_phase(left, right, grad, jobs, act):
        chain = plan.arrange(jobs)

        def body(ids, left_ref, out_ref):
            plan.beside(ids.index[0], chain, lambda: grad_body(left_ref, right, out_ref, act=act))
        pltpu.emit_pipeline(body, grid=(f // BLOCK,), in_specs=[pl.BlockSpec((rows, BLOCK), lambda i: (0, i))],
                            out_specs=[pl.BlockSpec((BLOCK, d), lambda i: (i, 0))], _explicit_indices=True)(left, grad)

    def up_phase(left, right, grad, jobs):
        chain = plan.arrange(jobs)

        def body(ids, right_ref, out_ref):
            plan.beside(ids.index[0], chain, lambda: grad_body(left, right_ref, out_ref, act=False))
        pltpu.emit_pipeline(body, grid=(f // BLOCK,), in_specs=[pl.BlockSpec((rows, BLOCK), lambda i: (0, i))],
                            out_specs=[pl.BlockSpec((d, BLOCK), lambda i: (0, i))], _explicit_indices=True)(right, grad)

    def e2_phase(jobs):
        chain = plan.arrange(jobs)

        def body(ids, q_ref):
            def work():
                e2 = lax.dot_general(q_ref[...], w3_v[...], DOT_NT, preferred_element_type=F32)
                res0[pl.ds(pl.multiple_of(ids.index[0] * TILE, TILE), TILE), :] = e2.astype(BF16)
            plan.beside(ids.index[0], chain, work)
        pltpu.emit_pipeline(body, grid=(rows // TILE,), in_specs=[pl.BlockSpec((TILE, f), lambda i: (i, 0))], _explicit_indices=True)(q3)

    def q1_phase(jobs):
        chain = plan.arrange(jobs)

        def body(ids, z_ref, q_ref):
            def work():
                e2 = res0[pl.ds(pl.multiple_of(ids.index[0] * TILE, TILE), TILE), :]
                for cols in col_chunks(f, 256):
                    e = lax.dot_general(e2, w2_v[cols, :], DOT_NT, preferred_element_type=F32).astype(BF16)
                    q_ref[:, cols] = (e.astype(F32) * gelu_grad(z_ref[:, cols].astype(F32))).astype(BF16)
            plan.beside(ids.index[0], chain, work)
        pltpu.emit_pipeline(body, grid=(rows // TILE,), in_specs=[pl.BlockSpec((TILE, f), lambda i: (i, 0))],
                            out_specs=[pl.BlockSpec((TILE, f), lambda i: (i, 0))], _explicit_indices=True)(z1, q1)

    def leave(red):
        for copy in red.mate_copies():
            copy.start()

    get_dy.start()
    get_dy.wait()
    get_h.start()
    get_w3.start()
    get_w2.start()
    down_phase(a3, res0, down4.grad, {}, False)
    leave(down4)
    get_h.wait()
    first4 = down4.firsts()
    up_phase(res1, q3, up3.grad, dict(zip((5, 6, 7, 8), first4)))
    leave(up3)
    get_x.start()
    get_w3.wait()
    first3 = up3.firsts()
    e2_phase(dict(zip((3, 4, 5, 6), first3)))
    second4 = down4.seconds()
    down_phase(z1, res0, down2.grad, dict(zip((1, 2, 3, 4), second4)), True)
    leave(down2)
    get_w2.wait()
    first2 = down2.firsts()
    second3 = up3.seconds()
    q1_phase(dict(zip((3, 4, 5, 6, 7), first2 + second3[:1])))
    get_x.wait()
    up_phase(res1, q1, up1.grad, dict(zip((0, 1, 2), second3[1:])))
    leave(up1)
    plan.run(down2.seconds())
    plan.run(up1.firsts())
    plan.run(up1.seconds())
    plan.flush()
    for red in reds:
        red.finish()


def reduce_gradients(a3, q3, z1, h, x, dy, w3, w2):
    rows, f = a3.shape
    d = x.shape[1]
    shapes = [jax.ShapeDtypeStruct((rows, f), BF16)]
    for up in (False, True, False, True):
        whole, width = ((d, f), f // 2) if up else ((f, d), d)
        part = (d if up else f // 2) // 4
        half = part // 2
        for shape in (whole, (2, 2, part, width), (2, 2, part, width), (2, half, width), (2, half, width),
                      (2, half, width), (2, half, width), (half, width), (half, width)):
            shapes.append(jax.ShapeDtypeStruct(shape, F32))
    up_block, down_block = pltpu.VMEM((d // 4, f // 2), F32), pltpu.VMEM((f // 8, d), F32)
    outs = pl.pallas_call(
        reduce_kernel,
        in_specs=[pl.BlockSpec(memory_space=pl.ANY)] * 8,
        out_specs=[pl.BlockSpec(memory_space=pl.ANY)] * len(shapes),
        out_shape=shapes,
        scratch_shapes=[
            pltpu.VMEM((rows, d), BF16), pltpu.VMEM((rows, d), BF16), pltpu.VMEM((d, f), BF16), pltpu.VMEM((f, d), BF16),
            up_block, up_block, up_block, down_block, down_block, down_block,
            pltpu.SemaphoreType.DMA((4, 10)), pltpu.SemaphoreType.DMA((4, 10)), pltpu.SemaphoreType.DMA((3,)), pltpu.SemaphoreType.DMA((5,)),
        ],
        compiler_params=pltpu.CompilerParams(vmem_limit_bytes=VMEM_LIMIT, collective_id=1, has_side_effects=True),
        cost_estimate=cost(12 * rows * d * f, 12 * rows * f),
        name="reduce_gradients",
    )(a3, q3, z1, h, x, dy, w3, w2)

    def shard(k):
        part_a, part_b, last_x, last_y = outs[1 + 9 * k + 5:10 + 9 * k]
        return jnp.concatenate([part_a[0] + last_x, part_b[0] + last_y], axis=0)

    return [shard(k) for k in range(4)]


def adam_update(master_arr, mom_arr, var_arr, grad_arr, clip_scale, lr_val):
    scaled = clip_scale * grad_arr
    new_mom = BETA_ONE * mom_arr + (1.0 - BETA_ONE) * scaled
    new_var = BETA_TWO * var_arr + (1.0 - BETA_TWO) * scaled * scaled
    mom_hat = new_mom / (1.0 - BETA_ONE ** STEP)
    var_hat = new_var / (1.0 - BETA_TWO ** STEP)
    new_master = master_arr - lr_val * mom_hat / (jnp.sqrt(var_hat) + ADAM_EPS)
    return new_master, new_mom, new_var


def solution(mesh):
    data_size = mesh.shape["data"]
    spec_rows = P("data", None)
    spec_wup = P(None, None, "model")
    spec_wdown = P(None, "model", None)
    spec_sup = P(None, "data", "model")
    spec_sdown = P(None, ("model", "data"), None)
    spec_scalar = P(None)

    def whole(own, dim):
        quarter = own.shape[1] // data_size
        mine = lax.dynamic_slice_in_dim(own, lax.axis_index("data") * quarter, quarter, 1)
        theirs = lax.ppermute(mine, "model", [(0, 1), (1, 0)])
        other = lax.all_gather(theirs, "data", axis=1, tiled=True)
        return jnp.concatenate([own, other], axis=dim)

    def local_step(act_in, grad_out, w_up, w_down, master_up, master_down, mom_up, mom_down, var_up, var_down, learn_rate, clip_norm):
        rows = act_in.shape[0] // 2
        start = lax.axis_index("model") * rows
        x = lax.dynamic_slice_in_dim(act_in, start, rows, 0)
        dy = lax.dynamic_slice_in_dim(grad_out, start, rows, 0)
        up, down = whole(w_up, 2), whole(w_down, 1)
        z1, h, a3, q3 = forward(x, dy, up[0], down[0], up[1], down[1])
        shard_w4, shard_w3, shard_w2, shard_w1 = reduce_gradients(a3, q3, z1, h, x, dy, up[1], down[0])
        grad_up_arr = jnp.stack([shard_w1, shard_w3]) / data_size
        grad_down_arr = jnp.stack([shard_w2, shard_w4]) / data_size
        sq_local = jnp.sum(grad_up_arr * grad_up_arr) + jnp.sum(grad_down_arr * grad_down_arr)
        norm_val = jnp.sqrt(lax.psum(sq_local, ("model", "data")))
        clip_scale = jnp.minimum(1.0, clip_norm[0] / (norm_val + NORM_EPS))
        lr_val = learn_rate[0]
        new_master_up, new_mom_up, new_var_up = adam_update(master_up, mom_up, var_up, grad_up_arr, clip_scale, lr_val)
        new_master_down, new_mom_down, new_var_down = adam_update(master_down, mom_down, var_down, grad_down_arr, clip_scale, lr_val)
        new_w_up = lax.all_gather(new_master_up.astype(BF16), "data", axis=1, tiled=True)
        new_w_down = lax.all_gather(new_master_down.astype(BF16), "data", axis=1, tiled=True)
        return (new_w_up, new_w_down, new_master_up, new_master_down, new_mom_up, new_mom_down, new_var_up, new_var_down, norm_val.reshape(1))

    return jax.shard_map(local_step, mesh=mesh, in_specs=(spec_rows, spec_rows, spec_wup, spec_wdown, spec_sup, spec_sdown, spec_sup, spec_sdown, spec_sup, spec_sdown, spec_scalar, spec_scalar), out_specs=(spec_wup, spec_wdown, spec_sup, spec_sdown, spec_sup, spec_sdown, spec_sup, spec_sdown, spec_scalar), check_vma=False)
```

time: 2130 us -> 718 us (0.34)
  blocking collectives: 1540 us -> 22.3 us
  Pallas kernels: 0 us -> 423 us
  matrix products: 392 us -> 0 us
  local copies, waits for them, and re-layouts: 32.2 us -> 70 us
  waiting for transfers between devices: 122 us -> 152 us
    psum x2 -> x0, blocking collectives: 1510 us -> none  [the longest x1 761 us: local_grads(): hid_two = lax.psum(hid_part, 'model').astype(jnp.bfloat16)]
    pallas_call x0 -> x2, Pallas kernels: none -> 423 us  [the longest x1 302 us: reduce_gradients(): pl.pallas_call(reduce_kernel, in_specs=[pl.BlockSpec(memory_space=pl.ANY)...]
    dot_general x10 -> x0, matrix products: 392 us -> none  [the longest x1 58.8 us: local_grads(): jnp.einsum('bd,fd->bf', dhid_two, w_down[0], preferred_element_type=jnp.f...]
    ppermute x0 -> x2, waiting for transfers between devices: none -> 62.6 us  [whole(): theirs = lax.ppermute(mine, 'model', [(0, 1), (1, 0)])]
    reduce_scatter x4 -> x0, waiting for transfers between devices: 61.8 us -> none  [the longest x1 50.4 us: local_step(): lax.psum_scatter(grad_w2, 'data', scatter_dimension=0, tiled=True)]
    all_gather x2 -> x4, waiting for transfers between devices: 59.9 us -> 89.5 us  [the longest x1 42.6 us: local_step(): lax.all_gather(new_master_up.astype(BF16), 'data', axis=1, tiled=True)]
  transfers between devices with their start and end apart: 6 -> 6, of which waited for: 4 -> 5; matrix products, arithmetic and copies ran while one was open for 11% -> 6% of each run, Pallas kernels for 0% -> 0%
where the time goes in v1:
time: 718 us; the launch traced here: 713 us
  Pallas kernels  423 us (59%)
  waiting for transfers between devices  152 us (21%)
  local copies, waits for them, and re-layouts  70 us (10%)
  blocking collectives  22.3 us (3%)
  other arithmetic  21.3 us (3%)
  between operations  18.8 us (3%)
    pallas_call x1, Pallas kernels, reduce_gradients(): pl.pallas_call(reduce_kernel, in_specs=[pl.BlockSpec(memory_space=pl.ANY)...  302 us
    pallas_call x1, Pallas kernels, forward(): pl.pallas_call(forward_body, grid=(rows // tile,), in_specs=[row_tile(til...  121 us
    ppermute x2, waiting for transfers between devices, whole(): theirs = lax.ppermute(mine, 'model', [(0, 1), (1, 0)])  62.6 us
    all_gather x1, waiting for transfers between devices, local_step(): lax.all_gather(new_master_up.astype(BF16), 'data', axis=1, tiled=True)  42.6 us
    all_gather x1, waiting for transfers between devices, local_step(): lax.all_gather(new_master_down.astype(BF16), 'data', axis=1, tiled=True)  35.3 us
    unnamed x44, local copies, waits for them, and re-layouts  24.6 us
    psum x1, blocking collectives, local_step(): norm_val = jnp.sqrt(lax.psum(sq_local, ('model', 'data')))  22.3 us
    squeeze x2, local copies, waits for them, and re-layouts, local_step(): z1, h, a3, q3 = forward(x, dy, up[0], down[0], up[1], down[1])  19.4 us
  transfers between devices with their start and end apart: 6, of which 5 were waited for; matrix products, arithmetic and copies ran while one was open for 6% of the time, Pallas kernels for 0%

profile of v1, /device:TPU:0, one launch (start us, length us, event | category | flops | bytes accessed | tf_op | source)
XLA Modules:
  0.0 712.8 jit_solution(13202547677279133922)
XLA Ops:
  7.2 1.5 constant_dynamic-slice_fusion
  8.7 3.4 collective-permute-start.1
  12.1 31.6 %collective-permute-done.1 = bf16[2,352,1024]{2,1,0:T(8,128)(2,1)S(1)} collective-permute-done((bf16[2,352,1024]{2,1,0:T(8,128)(2,1)S(1)}, bf16[2,352,1024]{2,1,0:T(8,128)(2,1)S(1)}, u32[]{:S(2)}, u32[]{:S(2)}) %collective-permute-start.1) | collective-permute-done | bytes 1441824 | tf_op jit(solution)/shard_map/ppermute | solution.py:405
  44.9 1.5 constant_dynamic-slice_fusion.1
  46.3 1.8 collective-permute-start
  48.1 31.0 %collective-permute-done = bf16[2,256,1408]{2,1,0:T(8,128)(2,1)S(1)} collective-permute-done((bf16[2,256,1408]{2,1,0:T(8,128)(2,1)S(1)}, bf16[2,256,1408]{2,1,0:T(8,128)(2,1)S(1)}, u32[]{:S(2)}, u32[]{:S(2)}) %collective-permute-start) | collective-permute-done | bytes 1441824 | tf_op jit(solution)/shard_map/ppermute | solution.py:405
  81.6 5.9 constant_dynamic-update-slice_fusion.3
  87.5 2.9 constant_dynamic-update-slice_fusion.1
  90.5 11.7 %constant_dynamic-slice_fusion.2 = (bf16[4096,1024]{1,0:T(8,128)(2,1)}, bf16[4096,1024]{1,0:T(8,128)(2,1)}) fusion(bf16[8192,1024]{1,0:T(8,128)(2,1)} %param.13, s32[]{:T(128)S(6)} %select_n.10, bf16[8192,1024]{1,0:T(8,128)(2,1)} %param.12), kind=kLoop, calls=%fused_computation.34 | loop fusion | bytes 33554436 | tf_op jit(solution)/shard_map/dynamic_slice | solution.py:413
  102.2 5.8 constant_dynamic-update-slice_fusion.2
  107.9 9.9 %slice_bitcast_fusion = (bf16[2816,1024]{1,0:T(8,128)(2,1)}, bf16[2816,1024]{1,0:T(8,128)(2,1)}) fusion(bf16[2,2816,1024]{2,1,0:T(8,128)(2,1)} %constant_dynamic-update-slice_fusion.2), kind=kLoop, calls=%fused_computation | loop fusion | bytes 23068672 | tf_op jit(solution)/shard_map/squeeze | solution.py:415
  117.8 11.7 %all-gather.5.cloned.1.call-done = bf16[2,1024,1408]{2,1,0:T(8,128)(2,1)} async-done(((bf16[2,256,1408]{2,1,0:T(8,128)(2,1)}), bf16[2,1024,1408]{2,1,0:T(8,128)(2,1)}) %all-gather.5.cloned.1.call-update) | async-done | bytes 5767184 | tf_op jit(solution)/shard_map/all_gather | solution.py:406
  129.5 5.6 constant_dynamic-update-slice_fusion
  135.0 9.5 %slice_bitcast_fusion.1 = (bf16[1024,2816]{1,0:T(8,128)(2,1)}, bf16[1024,2816]{1,0:T(8,128)(2,1)}) fusion(bf16[2,1024,2816]{2,1,0:T(8,128)(2,1)} %constant_dynamic-update-slice_fusion), kind=kLoop, calls=%fused_computation.1 | loop fusion | bytes 23068672 | tf_op jit(solution)/shard_map/squeeze | solution.py:415
  144.5 121.1 %forward.1 = (bf16[4096,2816]{1,0:T(8,128)(2,1)}, bf16[4096,1024]{1,0:T(8,128)(2,1)}, bf16[4096,2816]{1,0:T(8,128)(2,1)}, bf16[4096,2816]{1,0:T(8,128)(2,1)}) custom-call(bf16[4096,1024]{1,0:T(8,128)(2,1)} %get-tuple-element.62.x_ref.x, bf16[4096,1024]{1,0:T(8,128)(2,1)} %get-tuple-element.61.dy_ref.dy, bf16[1024,2816]{1,0:T(8,128)(2,1)} %get-tuple-element.60.w1_ref, ...), custom_call_target="tpu_custom_call" | custom-call | flops 94489280512 | bytes 69206016 | tf_op jit(solution)/shard_map/forward/pallas_call | solution.py:90
  265.6 301.9 %reduce_gradients.1 = (bf16[4096,2816]{1,0:T(8,128)(2,1)}, f32[2816,1024]{1,0:T(8,128)}, f32[2,2,352,1024]{3,2,1,0:T(8,128)}, f32[2,2,352,1024]{3,2,1,0:T(8,128)...) custom-call(bf16[4096,2816]{1,0:T(8,128)(2,1)} %get-tuple-element.29, ...), custom_call_target="tpu_custom_call" | custom-call | flops 141733920768 | bytes 138412032 | tf_op jit(solution)/shard_map/reduce_gradients/pallas_call | solution.py:361
  569.0 1.6 bitcast_add_fusion.2
  580.9 22.3 %psum.7 = f32[]{:T(128)} all-reduce(f32[]{:T(128)S(6)} %add.77), channel_id=1, replica_groups=mesh['model'=2,'data'=4] {'model','data'}, use_global_device_ids=true, to_apply=%region_2.0 | all-reduce | flops 1 | bytes 8 | tf_op jit(solution)/shard_map/psum | solution.py:420
  603.9 7.5 %fusion.2 = (bf16[2,352,1024]{2,1,0:T(8,128)(2,1)}, f32[2,352,1024]{2,1,0:T(8,128)}, f32[2,352,1024]{2,1,0:T(8,128)}, f32[2,352,1024]{2,1,0:T(8,128)}) fusion(f32[2,352,1024]{2,1,0:T(8,128)} %param.17, f32[]{:T(128)} %bitcast.17, f32[]{:T(128)S(6)} %mul.106, f32[1,352,1024]{2,1,0:T(8,128)} %copy-done, f32[1,352,1024]{2,1,0:T(8,128)S(1)} %maximum_bitcast_fusion.2, ...), kind=kLoop, calls=%fused_computation.36 | loop fusion | flops 10813440 | bytes 21626888 | tf_op jit(solution)/shard_map/convert_element_type | solution.py:426
  611.4 7.3 %fusion.4 = (bf16[2,256,1408]{2,1,0:T(8,128)(2,1)}, f32[2,256,1408]{2,1,0:T(8,128)}, f32[2,256,1408]{2,1,0:T(8,128)}, f32[2,256,1408]{2,1,0:T(8,128)}) fusion(f32[2,256,1408]{2,1,0:T(8,128)} %param.16, f32[]{:T(128)} %bitcast.17, f32[]{:T(128)S(6)} %mul.106, f32[1,256,1408]{2,1,0:T(8,128)} %copy-done.1, f32[1,256,1408]{2,1,0:T(8,128)S(1)} %maximum_bitcast_fusion, ...), kind=kLoop, calls=%fused_computation.37 | loop fusion | flops 10813440 | bytes 21626888 | tf_op jit(solution)/shard_map/convert_element_type | solution.py:425
  618.8 35.3 %all-gather.11.cloned.1.call-done = bf16[2,1408,1024]{2,1,0:T(8,128)(2,1)} async-done(((bf16[2,352,1024]{2,1,0:T(8,128)(2,1)}), bf16[2,1408,1024]{2,1,0:T(8,128)(2,1)}) %all-gather.11.cloned.1.call-update) | async-done | bytes 5767184 | tf_op jit(solution)/shard_map/all_gather | solution.py:426
  654.0 42.6 %all-gather.9.cloned.1.call-done = bf16[2,1024,1408]{2,1,0:T(8,128)(2,1)} async-done(((bf16[2,256,1408]{2,1,0:T(8,128)(2,1)}), bf16[2,1024,1408]{2,1,0:T(8,128)(2,1)}) %all-gather.9.cloned.1.call-update) | async-done | bytes 5767184 | tf_op jit(solution)/shard_map/all_gather | solution.py:425
  696.6 5.7 copy.27
  702.4 2.5 copy.28
  (64 shorter events, 12.7 us)
Async XLA Ops:
  7.2 95.0 %all-gather.7.cloned.1.call-start = ((), (), s32[]{:S(2)}) async-start(), calls=%async_computation.1 | async-start | bytes 7208960 | tf_op jit(solution)/shard_map/all_gather | solution.py:406
  8.7 35.0 %collective-permute-start.1 = (bf16[2,352,1024]{2,1,0:T(8,128)(2,1)S(1)}, bf16[2,352,1024]{2,1,0:T(8,128)(2,1)S(1)}, u32[]{:S(2)}, u32[]{:S(2)}) collective-permute-start(bf16[2,352,1024]{2,1,0:T(8,128)(2,1)S(1)} %constant_dynamic-slice_fusion), channel_id=1, source_target_pairs={{0,4},{4,0},{1,5},{5,1},{2,6},{6,2},{3,7},{7,3}} | collective-permute-start | bytes 4325384 | tf_op jit(solution)/shard_map/ppermute | solution.py:405
  44.8 84.7 %all-gather.5.cloned.1.call-start = ((), (), s32[]{:S(2)}) async-start(), calls=%async_computation | async-start | bytes 7208960 | tf_op jit(solution)/shard_map/all_gather | solution.py:406
  46.3 32.8 %collective-permute-start = (bf16[2,256,1408]{2,1,0:T(8,128)(2,1)S(1)}, bf16[2,256,1408]{2,1,0:T(8,128)(2,1)S(1)}, u32[]{:S(2)}, u32[]{:S(2)}) collective-permute-start(bf16[2,256,1408]{2,1,0:T(8,128)(2,1)S(1)} %constant_dynamic-slice_fusion.1), channel_id=1, source_target_pairs={{0,4},{4,0},{1,5},{5,1},{2,6},{6,2},{3,7},{7,3}} | collective-permute-start | bytes 4325384 | tf_op jit(solution)/shard_map/ppermute | solution.py:405
  80.2 573.8 %all-gather.11.cloned.1.call-start = ((), (), s32[]{:S(2)}) async-start(), calls=%async_computation.3 | async-start | bytes 7208960 | tf_op jit(solution)/shard_map/all_gather | solution.py:426
  81.6 6.0 slice-start
  81.6 5.9 slice-start.1
  569.0 1.7 copy-start.9
  569.0 2.0 copy-start.15
  570.6 1.2 copy-start.8
  570.6 1.7 copy-start.14
  572.4 1.5 copy-start.7
  572.4 2.1 copy-start.13
  572.5 2.7 copy-start
  572.5 2.1 copy-start.6
  572.5 2.6 copy-start.12
  574.6 1.2 copy-start.5
  574.6 1.7 copy-start.11
  575.2 1.2 copy-start.4
  575.2 1.7 copy-start.10
  577.1 1.1 copy-start.1
  611.4 85.2 %all-gather.9.cloned.1.call-start = ((), (), s32[]{:S(2)}) async-start(), calls=%async_computation.2 | async-start | bytes 7208960 | tf_op jit(solution)/shard_map/all_gather | solution.py:425
  696.6 5.7 slice-start.2
  696.6 5.7 slice-start.3
  (2 other events, 2.2 us)
Sparse Core Ops, SparseCore 0:
  44.9 41.7 all-gather.6
  88.8 40.5 all-gather.4
  611.5 42.4 all-gather.10
  656.0 40.5 all-gather.8

commit v2 on v1

v2 whole, which is shorter than its diff:
```python
import functools

import jax
import jax.numpy as jnp
from jax import lax
from jax.experimental import pallas as pl
from jax.experimental.pallas import tpu as pltpu
from jax.sharding import PartitionSpec as P

STEP = 10
BETA_ONE = 0.9
BETA_TWO = 0.95
ADAM_EPS = 1e-8
NORM_EPS = 1e-6
GELU_A = 0.7978845608028654
GELU_B = GELU_A * 0.044715
BF16 = jnp.bfloat16
F32 = jnp.float32
DOT_NT = (((1,), (1,)), ((), ()))
DOT_TN = (((0,), (0,)), ((), ()))
VMEM_LIMIT = 60 * 2**20


def gelu(z):
    half = 0.5 * z
    return half + half * jnp.tanh(z * (z * z * GELU_B + GELU_A))


def gelu_grad(z):
    sq = z * z
    sig = 0.5 * jnp.tanh(z * (sq * GELU_B + GELU_A)) + 0.5
    return sig + z * (sq * (6.0 * GELU_B) + 2.0 * GELU_A) * (sig - sig * sig)


def gelu_both(z):
    sq = z * z
    sig = 0.5 * jnp.tanh(z * (sq * GELU_B + GELU_A)) + 0.5
    act = z * sig
    return act, sig + (act - act * sig) * (sq * (6.0 * GELU_B) + 2.0 * GELU_A)


def col_chunks(width, step):
    return [slice(lo, min(lo + step, width)) for lo in range(0, width, step)]


def grad_body(left_ref, right_ref, out_ref, *, act):
    left = left_ref[...]
    if act:
        left = gelu(left.astype(F32)).astype(BF16)
    out_ref[...] = lax.dot_general(left, right_ref[...], DOT_TN, preferred_element_type=F32)


def cost(flops, moved):
    return pl.CostEstimate(flops=flops, bytes_accessed=moved, transcendentals=0)


MESH = pl.DeviceIdType.MESH
TILE = 512
BLOCK = 256


class Lanes:
    def __init__(self):
        data = lax.axis_index("data")
        self.model = lax.axis_index("model")
        self.x, self.core = data // 2, data % 2
        self.mate = {"data": 2 * self.x + (1 - self.core)}
        self.over_x = {"data": 2 * (1 - self.x) + self.core}
        self.over_y = {"model": 1 - self.model}
        self.near = (self.mate, self.over_x, self.over_y)
        self.place = 4 * self.model + data

    def others(self):
        places = [(self.place + step) % 8 for step in range(1, 8)]
        return [{"model": place // 4, "data": place % 4} for place in places]

    def shard(self, far, core):
        return 2 * ((self.x + far) % 2) + core


def greet(peers):
    barrier = pltpu.get_barrier_semaphore()
    for peer in peers:
        pl.semaphore_signal(barrier, inc=1, device_id=peer, device_id_type=MESH)
    pl.semaphore_wait(barrier, len(peers))


class Gather:
    def __init__(self, lanes, own, whole, up, send, recv):
        self.send, self.recv = send, recv
        data = lanes.shard(0, lanes.core)
        half = own.shape[1] if up else own.shape[0]
        part = own.shape[0] // 4

        def quarter(shard):
            if up:
                return whole.at[pl.ds(shard * part, part), pl.ds(half, half)]
            return whole.at[pl.ds(half + shard * part, part), :]

        near, far = quarter(data), quarter(lanes.shard(1, lanes.core))
        self.over_y = self.remote(0, own.at[pl.ds(data * part, part), :], near, lanes.over_y)
        self.over_x = self.remote(1, near, near, lanes.over_x)
        self.near = self.remote(2, near, near, lanes.mate)
        self.far = self.remote(3, far, far, lanes.mate)

    def remote(self, slot, src, dst, peer):
        return pltpu.make_async_remote_copy(src, dst, self.send.at[slot], self.recv.at[slot], device_id=peer, device_id_type=MESH)

    def start(self):
        self.over_y.start()

    def pass_near(self):
        self.over_y.wait_recv()
        self.over_x.start()
        self.near.start()

    def pass_far(self):
        self.over_x.wait_recv()
        self.far.start()

    def arrived(self):
        self.near.wait_recv()
        self.far.wait_recv()

    def sent(self):
        for copy in (self.over_y, self.over_x, self.near, self.far):
            copy.wait_send()


def at_steps(step, events):
    for at, event in events.items():
        @pl.when(step == at)
        def _(event=event):
            event()


def forward_kernel(act, grad, w_up, w_down, z1, h, a3, q3, e3, w3_out, w2_out, w1_v, w2_v, w3_v, w4_v, a1_v, send, recv, fetch):
    lanes = Lanes()
    greet(lanes.near)
    owns = [(w_up.at[0], w1_v, True), (w_down.at[0], w2_v, False), (w_up.at[1], w3_v, True), (w_down.at[1], w4_v, False)]
    gathers = [Gather(lanes, own, whole, up, send.at[k], recv.at[k]) for k, (own, whole, up) in enumerate(owns)]
    g1, g2, g3, g4 = gathers
    for gather in gathers:
        gather.start()
    half = w_up.shape[2]
    loads = []
    for k, (own, whole, up) in enumerate(owns):
        place = whole.at[:, pl.ds(0, half)] if up else whole.at[pl.ds(0, half), :]
        loads.append(pltpu.make_async_copy(own, place, fetch.at[k]))
    for k in (0, 3, 1, 2):
        loads[k].start()
    rows, d = h.shape
    f = z1.shape[1]
    steps = rows // TILE
    first = lanes.model * steps
    mine = pl.BlockSpec((TILE, d), lambda i: (first + i, 0))
    slim = pl.BlockSpec((TILE, d), lambda i: (i, 0))
    wide = pl.BlockSpec((TILE, f), lambda i: (i, 0))
    left = pl.BlockSpec((TILE, half), lambda i: (i, 0))
    right = pl.BlockSpec((TILE, half), lambda i: (i, 1))

    def own_body(ids, x_ref, dy_ref, z_ref, e_ref):
        at_steps(ids.index[0], {5: g1.pass_near})
        z_ref[...] = jnp.dot(x_ref[...], w1_v[:, :half], preferred_element_type=F32).astype(BF16)
        e_ref[...] = lax.dot_general(dy_ref[...], w4_v[:half, :], DOT_NT, preferred_element_type=F32).astype(BF16)

    def other_body(ids, x_ref, z_ref):
        def pass_on():
            g2.pass_far()
            g3.pass_near()

        at_steps(ids.index[0], {7: pass_on})
        z_ref[...] = jnp.dot(x_ref[...], w1_v[:, half:], preferred_element_type=F32).astype(BF16)

    def h_body(ids, z_ref, h_ref):
        def pass_on():
            g4.pass_near()
            g3.pass_far()

        at_steps(ids.index[0], {4: pass_on})
        for cols in col_chunks(f, 256):
            a1_v[:, cols] = gelu(z_ref[:, cols].astype(F32)).astype(BF16)
        h_ref[...] = jnp.dot(a1_v[...], w2_v[...], preferred_element_type=F32).astype(BF16)

    def last_body(ids, h_ref, dy_ref, e_ref, a_ref, q_ref):
        hid, dy = h_ref[...], dy_ref[...]
        for lo, hi in halves(half):
            cols = slice(lo, hi)
            z = jnp.dot(hid, w3_v[:, cols], preferred_element_type=F32).astype(BF16)
            if hi <= half:
                e = e_ref[:, cols]
            else:
                e = lax.dot_general(dy, w4_v[cols, :], DOT_NT, preferred_element_type=F32).astype(BF16)
            act_val, slope = gelu_both(z.astype(F32))
            a_ref[:, cols] = act_val.astype(BF16)
            q_ref[:, cols] = (e.astype(F32) * slope).astype(BF16)

    def pipe(body, ins, outs, refs):
        pltpu.emit_pipeline(body, grid=(steps,), in_specs=ins, out_specs=outs, _explicit_indices=True)(*refs)

    loads[0].wait()
    loads[3].wait()
    pipe(own_body, [mine, mine], [left, left], (act, grad, z1, e3))
    loads[1].wait()
    loads[2].wait()
    g2.pass_near()
    g1.pass_far()
    g1.arrived()
    pipe(other_body, [mine], [right], (act, z1))
    g2.arrived()
    save2 = pltpu.make_async_copy(w2_v, w2_out, fetch.at[0])
    save2.start()
    pipe(h_body, [wide], [slim], (z1, h))
    g4.pass_far()
    g3.arrived()
    g4.arrived()
    save3 = pltpu.make_async_copy(w3_v, w3_out, fetch.at[1])
    save3.start()
    pipe(last_body, [slim, mine, left], [wide, wide], (h, grad, e3, a3, q3))
    save2.wait()
    save3.wait()
    for gather in gathers:
        gather.sent()


def halves(half):
    return [(base + cols.start, base + cols.stop) for base in (0, half) for cols in col_chunks(half, 256)]


def forward(act, grad, w_up, w_down):
    d, half = w_up.shape[1:]
    rows, f = act.shape[0] // 2, 2 * half
    wide, slim, own = (jax.ShapeDtypeStruct((rows, n), BF16) for n in (f, d, half))
    up, down = (d, f), (f, d)
    outs = [wide, slim, wide, wide, own, jax.ShapeDtypeStruct(up, BF16), jax.ShapeDtypeStruct(down, BF16)]
    z1, h, a3, q3, _, w3, w2 = pl.pallas_call(
        forward_kernel,
        in_specs=[pl.BlockSpec(memory_space=pl.ANY)] * 4,
        out_specs=[pl.BlockSpec(memory_space=pl.ANY)] * len(outs),
        out_shape=outs,
        scratch_shapes=[pltpu.VMEM(up, BF16), pltpu.VMEM(down, BF16), pltpu.VMEM(up, BF16), pltpu.VMEM(down, BF16), pltpu.VMEM((TILE, f), BF16),
                        pltpu.SemaphoreType.DMA((4, 4)), pltpu.SemaphoreType.DMA((4, 4)), pltpu.SemaphoreType.DMA((4,))],
        compiler_params=pltpu.CompilerParams(vmem_limit_bytes=VMEM_LIMIT, collective_id=0, has_side_effects=True),
        cost_estimate=cost(8 * rows * d * f, 8 * rows * f),
        name="forward",
    )(act, grad, w_up, w_down)
    return z1, h, a3, q3, w3, w2


class Reducer:
    def __init__(self, lanes, up, bufs, send, recv, scratch, local, squares):
        self.lanes, self.up, self.send, self.recv, self.local = lanes, up, send, recv, local
        self.squares = squares
        self.grad, self.mated, self.chip, self.from_y, self.from_x, self.part_a, self.part_b, self.last_x, self.last_y, self.shard = bufs
        self.left, self.right, self.out = scratch
        self.rows = self.left.shape[0] // 2
        self.copies = {}
        for half in range(2):
            self.leave(half)

    def block(self, half, shard):
        if self.up:
            rows, width = 2 * self.rows, self.left.shape[1]
            return self.grad.at[pl.ds(shard * rows, rows), pl.ds(half * width, width)]
        rows = 2 * self.rows
        return self.grad.at[pl.ds(half * 4 * rows + shard * rows, rows), :]

    def remote(self, slot, src, dst, peer):
        copy = pltpu.make_async_remote_copy(src, dst, self.send.at[slot], self.recv.at[slot], device_id=peer, device_id_type=MESH)
        self.copies[slot] = copy
        return copy

    def leave(self, half):
        lanes = self.lanes
        for far in range(2):
            shard = lanes.shard(far, 1 - lanes.core)
            self.remote(2 * half + far, self.block(half, shard), self.mated.at[half, far], lanes.mate)

    def go(self, half):
        for far in range(2):
            self.copies[2 * half + far].start()

    def first(self, half, far):
        lanes, rows = self.lanes, self.rows
        chip = self.chip.at[half, far]
        sends = []
        if half == 1:
            sends.append(self.remote(4 + far, chip.at[pl.ds(0, rows)], self.from_y.at[far], lanes.over_y))
        if far == 1:
            sends.append(self.remote(6 + half, chip.at[pl.ds(rows, rows)], self.from_x.at[half], lanes.over_x))
        return Job(self, self.block(half, lanes.shard(far, lanes.core)), self.mated.at[half, far], chip, 2 * rows, (2 * half + far,), sends)

    def second_a(self, far):
        dst = self.part_a.at[far]
        sends = [self.remote(8, dst, self.last_x, self.lanes.over_x)] if far == 1 else []
        return Job(self, self.chip.at[0, far].at[pl.ds(0, self.rows)], self.from_y.at[far], dst, self.rows, (4 + far,), sends)

    def second_b(self, half):
        dst = self.part_b.at[half]
        sends = [self.remote(9, dst, self.last_y, self.lanes.over_y)] if half == 1 else []
        return Job(self, self.chip.at[half, 0].at[pl.ds(self.rows, self.rows)], self.from_x.at[half], dst, self.rows, (6 + half,), sends)

    def thirds(self):
        top, bottom = self.shard.at[pl.ds(0, self.rows)], self.shard.at[pl.ds(self.rows, self.rows)]
        return [Job(self, self.part_a.at[0], self.last_x, top, self.rows, (8,), [], True),
                Job(self, self.part_b.at[0], self.last_y, bottom, self.rows, (9,), [], True)]

    def firsts(self):
        return [self.first(1, 1), self.first(1, 0), self.first(0, 1), self.first(0, 0)]

    def seconds(self):
        return [self.second_a(1), self.second_b(1), self.second_a(0), self.second_b(0)]

    def finish(self):
        for slot in range(10):
            self.copies[slot].wait_send()


class Job:
    def __init__(self, owner, left, right, dst, rows, arrivals, sends, last=False):
        view = lambda ref: ref.at[pl.ds(0, rows)]
        self.owner, self.arrivals, self.sends, self.last = owner, arrivals, sends, last
        self.bufs = view(owner.left), view(owner.right), view(owner.out)
        self.loads = [pltpu.make_async_copy(src, buf, owner.local.at[k]) for k, (src, buf) in enumerate(zip((left, right), self.bufs))]
        self.store = pltpu.make_async_copy(self.bufs[2], dst, owner.local.at[2])

    def start(self):
        for slot in self.arrivals:
            self.owner.copies[slot].wait_recv()
        for load in self.loads:
            load.start()

    def add(self):
        for load in self.loads:
            load.wait()
        left, right, out = self.bufs
        if self.last:
            value = (left[...] + right[...]) * 0.25
            out[...] = value
            self.owner.squares[...] += jnp.sum((value * value).reshape(-1, 8, value.shape[1]), axis=0)
        else:
            out[...] = left[...] + right[...]
        self.store.start()

    def done(self):
        self.store.wait()
        for copy in self.sends:
            copy.start()


class Plan:
    def __init__(self):
        self.pending = None

    def arrange(self, jobs):
        chain = []
        for at in sorted(jobs):
            chain.append((at, self.pending, jobs[at]))
            self.pending = jobs[at]
        return chain

    @staticmethod
    def beside(step, chain, work):
        for at, old, job in chain:
            @pl.when(step == at)
            def _(old=old, job=job):
                if old is not None:
                    old.done()
                job.start()
        work()
        for at, old, job in chain:
            @pl.when(step == at)
            def _(job=job):
                job.add()

    def run(self, jobs):
        for job in jobs:
            if self.pending is not None:
                self.pending.done()
            job.start()
            job.add()
            self.pending = job

    def flush(self):
        if self.pending is not None:
            self.pending.done()
        self.pending = None


def reduce_kernel(a3, q3, z1, h, act_in, grad_out, w3, w2, *refs):
    outs, scratch = refs[:42], refs[42:]
    q1, norm_out = outs[:2]
    bufs = [outs[2 + 10 * k:12 + 10 * k] for k in range(4)]
    res0, res1, w3_v, w2_v, up_l, up_r, up_o, dn_l, dn_r, dn_o, up_sq, dn_sq, mine_sq, all_sq, send, recv, local, fetch, sq_send, sq_recv = scratch
    lanes = Lanes()
    greet(lanes.others())
    reds = [Reducer(lanes, up, bufs[k], send.at[k], recv.at[k], (up_l, up_r, up_o) if up else (dn_l, dn_r, dn_o), local,
                    up_sq if up else dn_sq)
            for k, up in enumerate((False, True, False, True))]
    down4, up3, down2, up1 = reds
    rows, f = a3.shape
    d = h.shape[1]
    mine = pl.ds(lanes.model * rows, rows)
    x, dy = act_in.at[mine, :], grad_out.at[mine, :]
    load = lambda src, dst, k: pltpu.make_async_copy(src, dst, fetch.at[k])
    get_dy, get_h, get_x, get_w3, get_w2 = load(dy, res0, 0), load(h, res1, 1), load(x, res1, 2), load(w3, w3_v, 3), load(w2, w2_v, 4)
    plan = Plan()
    up_sq[...] = jnp.zeros_like(up_sq)
    dn_sq[...] = jnp.zeros_like(dn_sq)

    def down_phase(left, right, grad, jobs, act):
        chain = plan.arrange(jobs)

        def body(ids, left_ref, out_ref):
            plan.beside(ids.index[0], chain, lambda: grad_body(left_ref, right, out_ref, act=act))
        pltpu.emit_pipeline(body, grid=(f // BLOCK,), in_specs=[pl.BlockSpec((rows, BLOCK), lambda i: (0, i))],
                            out_specs=[pl.BlockSpec((BLOCK, d), lambda i: (i, 0))], _explicit_indices=True)(left, grad)

    def up_phase(left, right, grad, jobs, events=None, skip=0):
        chain, blocks = plan.arrange(jobs), f // BLOCK

        def body(ids, right_ref, out_ref):
            at_steps(ids.index[0], events or {})
            plan.beside(ids.index[0], chain, lambda: grad_body(left, right_ref, out_ref, act=False))
        place = lambda i: (0, (i + skip) % blocks)
        pltpu.emit_pipeline(body, grid=(blocks,), in_specs=[pl.BlockSpec((rows, BLOCK), place)],
                            out_specs=[pl.BlockSpec((d, BLOCK), place)], _explicit_indices=True)(right, grad)

    def e2_phase(jobs):
        chain = plan.arrange(jobs)

        def body(ids, q_ref):
            def work():
                e2 = lax.dot_general(q_ref[...], w3_v[...], DOT_NT, preferred_element_type=F32)
                res0[pl.ds(pl.multiple_of(ids.index[0] * TILE, TILE), TILE), :] = e2.astype(BF16)
            plan.beside(ids.index[0], chain, work)
        pltpu.emit_pipeline(body, grid=(rows // TILE,), in_specs=[pl.BlockSpec((TILE, f), lambda i: (i, 0))], _explicit_indices=True)(q3)

    def q1_phase(jobs):
        chain = plan.arrange(jobs)

        def body(ids, z_ref, q_ref):
            def work():
                e2 = res0[pl.ds(pl.multiple_of(ids.index[0] * TILE, TILE), TILE), :]
                for cols in col_chunks(f, 256):
                    e = lax.dot_general(e2, w2_v[cols, :], DOT_NT, preferred_element_type=F32).astype(BF16)
                    q_ref[:, cols] = (e.astype(F32) * gelu_grad(z_ref[:, cols].astype(F32))).astype(BF16)
            plan.beside(ids.index[0], chain, work)
        pltpu.emit_pipeline(body, grid=(rows // TILE,), in_specs=[pl.BlockSpec((TILE, f), lambda i: (i, 0))],
                            out_specs=[pl.BlockSpec((TILE, f), lambda i: (i, 0))], _explicit_indices=True)(z1, q1)

    def leave(red):
        red.go(0)
        red.go(1)

    get_dy.start()
    get_dy.wait()
    get_h.start()
    get_w3.start()
    get_w2.start()
    down_phase(a3, res0, down4.grad, {}, False)
    leave(down4)
    get_h.wait()
    first4 = down4.firsts()
    up_phase(res1, q3, up3.grad, dict(zip((5, 6, 7, 8), first4)))
    leave(up3)
    get_x.start()
    get_w3.wait()
    first3 = up3.firsts()
    e2_phase(dict(zip((3, 4, 5, 6), first3)))
    second4 = down4.seconds()
    down_phase(z1, res0, down2.grad, dict(zip((1, 2, 3, 4), second4)), True)
    leave(down2)
    get_w2.wait()
    first2 = down2.firsts()
    second3 = up3.seconds()
    q1_phase(dict(zip(range(8), second3[:2] + first2 + second3[2:])))
    get_x.wait()
    second2 = down2.seconds()
    first1 = up1.firsts()
    beside1 = down4.thirds() + up3.thirds() + second2 + first1[:1]
    up_phase(res1, q1, up1.grad, dict(zip((0, 1, 2, 3, 5, 6, 8, 9, 10), beside1)), {7: lambda: up1.go(1)}, f // 2 // BLOCK)
    up1.go(0)
    plan.run(first1[1:])
    plan.run(down2.thirds())
    plan.run(up1.seconds())
    plan.run(up1.thirds())
    plan.flush()
    total = dn_sq[:, :128] + up_sq[:, :128]
    for cols in col_chunks(d, 128)[1:]:
        total += dn_sq[:, cols]
    for cols in col_chunks(f // 2, 128)[1:]:
        total += up_sq[:, cols]
    mine_sq[...] = total
    copies = []
    for k, peer in enumerate(lanes.others()):
        copy = pltpu.make_async_remote_copy(mine_sq, all_sq.at[lanes.place], sq_send.at[k], sq_recv.at[k], device_id=peer, device_id_type=MESH)
        copy.start()
        copies.append(copy)
    own = pltpu.make_async_copy(mine_sq, all_sq.at[lanes.place], local.at[0])
    own.start()
    own.wait()
    for red in reds:
        red.finish()
    for copy in copies:
        copy.wait()
    norm_out[...] = jnp.sum(all_sq[...], axis=0)


def reduce_gradients(a3, q3, z1, h, act_in, grad_out, w3, w2):
    rows, f = a3.shape
    d = h.shape[1]
    shapes = [jax.ShapeDtypeStruct((rows, f), BF16), jax.ShapeDtypeStruct((8, 128), F32)]
    for up in (False, True, False, True):
        whole, width = ((d, f), f // 2) if up else ((f, d), d)
        part = (d if up else f // 2) // 4
        half = part // 2
        for shape in (whole, (2, 2, part, width), (2, 2, part, width), (2, half, width), (2, half, width),
                      (2, half, width), (2, half, width), (half, width), (half, width), (part, width)):
            shapes.append(jax.ShapeDtypeStruct(shape, F32))
    up_block, down_block = pltpu.VMEM((d // 4, f // 2), F32), pltpu.VMEM((f // 8, d), F32)
    outs = pl.pallas_call(
        reduce_kernel,
        in_specs=[pl.BlockSpec(memory_space=pl.ANY)] * 8,
        out_specs=[pl.BlockSpec(memory_space=pltpu.VMEM if k == 1 else pl.ANY) for k in range(len(shapes))],
        out_shape=shapes,
        scratch_shapes=[
            pltpu.VMEM((rows, d), BF16), pltpu.VMEM((rows, d), BF16), pltpu.VMEM((d, f), BF16), pltpu.VMEM((f, d), BF16),
            up_block, up_block, up_block, down_block, down_block, down_block,
            pltpu.VMEM((8, f // 2), F32), pltpu.VMEM((8, d), F32), pltpu.VMEM((8, 128), F32), pltpu.VMEM((8, 8, 128), F32),
            pltpu.SemaphoreType.DMA((4, 10)), pltpu.SemaphoreType.DMA((4, 10)), pltpu.SemaphoreType.DMA((3,)), pltpu.SemaphoreType.DMA((5,)),
            pltpu.SemaphoreType.DMA((7,)), pltpu.SemaphoreType.DMA((7,)),
        ],
        compiler_params=pltpu.CompilerParams(vmem_limit_bytes=VMEM_LIMIT, collective_id=1, has_side_effects=True),
        cost_estimate=cost(12 * rows * d * f, 12 * rows * f),
        name="reduce_gradients",
    )(a3, q3, z1, h, act_in, grad_out, w3, w2)

    return [outs[11 + 10 * k] for k in range(4)], jnp.sum(outs[1])


def adam_update(master_arr, mom_arr, var_arr, grad_arr, clip_scale, lr_val):
    scaled = clip_scale * grad_arr
    new_mom = BETA_ONE * mom_arr + (1.0 - BETA_ONE) * scaled
    new_var = BETA_TWO * var_arr + (1.0 - BETA_TWO) * scaled * scaled
    mom_hat = new_mom / (1.0 - BETA_ONE ** STEP)
    var_hat = new_var / (1.0 - BETA_TWO ** STEP)
    new_master = master_arr - lr_val * mom_hat / (jnp.sqrt(var_hat) + ADAM_EPS)
    return new_master, new_mom, new_var


def solution(mesh):
    data_size = mesh.shape["data"]
    spec_rows = P("data", None)
    spec_wup = P(None, None, "model")
    spec_wdown = P(None, "model", None)
    spec_sup = P(None, "data", "model")
    spec_sdown = P(None, ("model", "data"), None)
    spec_scalar = P(None)

    def spread(own):
        over_x, over_core = [(i, i ^ 2) for i in range(4)], [(i, i ^ 1) for i in range(4)]
        far = lax.ppermute(own, "data", over_x)
        mate = lax.ppermute(own, "data", over_core)
        far_mate = lax.ppermute(far, "data", over_core)
        data, part = lax.axis_index("data"), own.shape[1]
        out = jnp.broadcast_to(own[:1, :1, :1], (own.shape[0], data_size * part, own.shape[2]))
        for flip, rows in ((0, own), (1, mate), (2, far), (3, far_mate)):
            out = lax.dynamic_update_slice_in_dim(out, rows, (data ^ flip) * part, 1)
        return out

    def local_step(act_in, grad_out, w_up, w_down, master_up, master_down, mom_up, mom_down, var_up, var_down, learn_rate, clip_norm):
        z1, h, a3, q3, w3, w2 = forward(act_in, grad_out, w_up, w_down)
        (shard_w4, shard_w3, shard_w2, shard_w1), squares = reduce_gradients(a3, q3, z1, h, act_in, grad_out, w3, w2)
        grad_up_arr = jnp.stack([shard_w1, shard_w3])
        grad_down_arr = jnp.stack([shard_w2, shard_w4])
        norm_val = jnp.sqrt(squares)
        clip_scale = jnp.minimum(1.0, clip_norm[0] / (norm_val + NORM_EPS))
        lr_val = learn_rate[0]
        new_master_up, new_mom_up, new_var_up = adam_update(master_up, mom_up, var_up, grad_up_arr, clip_scale, lr_val)
        new_master_down, new_mom_down, new_var_down = adam_update(master_down, mom_down, var_down, grad_down_arr, clip_scale, lr_val)
        new_w_up, new_w_down = spread(new_master_up.astype(BF16)), spread(new_master_down.astype(BF16))
        return (new_w_up, new_w_down, new_master_up, new_master_down, new_mom_up, new_mom_down, new_var_up, new_var_down, norm_val.reshape(1))

    return jax.shard_map(local_step, mesh=mesh, in_specs=(spec_rows, spec_rows, spec_wup, spec_wdown, spec_sup, spec_sdown, spec_sup, spec_sdown, spec_sup, spec_sdown, spec_scalar, spec_scalar), out_specs=(spec_wup, spec_wdown, spec_sup, spec_sdown, spec_sup, spec_sdown, spec_sup, spec_sdown, spec_scalar), check_vma=False)
```

time: 718 us -> 565 us (0.79)
  waiting for transfers between devices: 152 us -> 56.6 us
  local copies, waits for them, and re-layouts: 70 us -> 18.3 us
  Pallas kernels: 423 us -> 464 us
  blocking collectives: 22.3 us -> 0 us
  between operations: 18.8 us -> 4.42 us
  other arithmetic: 21.3 us -> 14.1 us
    all_gather x4 -> x0, waiting for transfers between devices: 89.5 us -> none  [the longest x1 42.6 us: local_step(): lax.all_gather(new_master_up.astype(BF16), 'data', axis=1, tiled=True)]
    pallas_call x1, Pallas kernels: 121 us -> 162 us  [forward(): pl.pallas_call(forward_kernel, in_specs=[pl.BlockSpec(memory_space=pl.ANY...]
    psum x1 -> x0, blocking collectives: 22.3 us -> none  [local_step(): norm_val = jnp.sqrt(lax.psum(sq_local, ('model', 'data')))]
    unnamed x44 -> x14, local copies, waits for them, and re-layouts: 24.6 us -> 4.18 us
    squeeze x2 -> x0, local copies, waits for them, and re-layouts: 19.4 us -> none  [local_step(): z1, h, a3, q3 = forward(x, dy, up[0], down[0], up[1], down[1])]
    dynamic_slice x3 -> x0, local copies, waits for them, and re-layouts: 14.6 us -> none  [the longest x1 11.7 us: local_step(): dy = lax.dynamic_slice_in_dim(grad_out, start, rows, 0)]
    concatenate x2 -> x0, local copies, waits for them, and re-layouts: 11.3 us -> none  [whole(): return jnp.concatenate([own, other], axis=dim)]
    dynamic_update_slice x0 -> x8, local copies, waits for them, and re-layouts: none -> 10.7 us  [spread(): out = lax.dynamic_update_slice_in_dim(out, rows, (data ^ flip) * part, 1)]
  transfers between devices with their start and end apart: 6 -> 6, of which waited for: 5 -> 2; matrix products, arithmetic and copies ran while one was open for 6% -> 3% of each run, Pallas kernels for 0% -> 0%
where the time goes in v2:
time: 565 us; the launch traced here: 560 us
  Pallas kernels  464 us (82%)
  waiting for transfers between devices  56.6 us (10%)
  local copies, waits for them, and re-layouts  18.3 us (3%)
  other arithmetic  14.1 us (2%)
    pallas_call x1, Pallas kernels, reduce_gradients(): pl.pallas_call(reduce_kernel, in_specs=[pl.BlockSpec(memory_space=pl.ANY)...  302 us
    pallas_call x1, Pallas kernels, forward(): pl.pallas_call(forward_kernel, in_specs=[pl.BlockSpec(memory_space=pl.ANY...  162 us
    ppermute x2, waiting for transfers between devices, spread(): far = lax.ppermute(own, 'data', over_x)  56.6 us
  transfers between devices with their start and end apart: 6, of which 2 were waited for; matrix products, arithmetic and copies ran while one was open for 3% of the time, Pallas kernels for 0%

profile of v2, /device:TPU:0, one launch (start us, length us, event | category | flops | bytes accessed | tf_op | source)
XLA Modules:
  0.0 559.7 jit_solution(13502689903669209859)
XLA Ops:
  0.6 162.4 %forward.1 = (bf16[4096,2816]{1,0:T(8,128)(2,1)}, bf16[4096,1024]{1,0:T(8,128)(2,1)}, bf16[4096,2816]{1,0:T(8,128)(2,1)}, bf16[4096,2816]{1,0:T(8,128)(2,1)}, bf...) custom-call(bf16[8192,1024]{1,0:T(8,128)(2,1)} %act_in.1, ...), custom_call_target="tpu_custom_call" | custom-call | flops 94489280512 | bytes 92274688 | tf_op jit(solution)/shard_map/forward/pallas_call | solution.py:236
  163.1 302.0 %reduce_gradients.1 = (bf16[4096,2816]{1,0:T(8,128)(2,1)}, f32[8,128]{1,0:T(8,128)}, f32[2816,1024]{1,0:T(8,128)}, f32[2,2,352,1024]{3,2,1,0:T(8,128)}, f32[2,2,...) custom-call(bf16[4096,2816]{1,0:T(8,128)(2,1)} %get-tuple-element.20, ...), custom_call_target="tpu_custom_call" | custom-call | flops 141733920768 | bytes 138412032 | tf_op jit(solution)/shard_map/reduce_gradients/pallas_call | solution.py:522
  465.1 1.3 reduce_sum.9
  468.5 8.3 %fusion.2 = (bf16[2,352,1024]{2,1,0:T(8,128)(2,1)S(1)}, f32[2,352,1024]{2,1,0:T(8,128)}, f32[2,352,1024]{2,1,0:T(8,128)}, f32[2,352,1024]{2,1,0:T(8,128)}) fusion(f32[2,352,1024]{2,1,0:T(8,128)} %param.17, f32[]{:T(128)} %bitcast.3, f32[1,352,1024]{2,1,0:T(8,128)} %bitcast.12, f32[1,352,1024]{2,1,0:T(8,128)} %bitcast.13, f32[]{:T(128)S(6)} %min_shard_map.3, ...), kind=kLoop, calls=%fused_computation.18 | loop fusion | flops 10813440 | bytes 21626888 | tf_op jit(solution)/shard_map/convert_element_type | solution.py:582
  476.8 0.6 collective-permute-start.4
  477.5 0.9 copy-done.4
  478.3 0.4 copy-done.5
  478.7 0.4 copy-done.6
  479.1 4.4 fusion.4
  483.5 0.6 collective-permute-start.1
  484.2 0.5 collective-permute-start
  484.7 26.6 %collective-permute-done.4 = bf16[2,352,1024]{2,1,0:T(8,128)(2,1)} collective-permute-done((bf16[2,352,1024]{2,1,0:T(8,128)(2,1)S(1)}, bf16[2,352,1024]{2,1,0:T(8,128)(2,1)}, u32[]{:S(2)}, u32[]{:S(2)}) %collective-permute-start.4) | collective-permute-done | bytes 1441824 | tf_op jit(solution)/shard_map/ppermute | solution.py:563
  511.3 30.0 %collective-permute-done.1 = bf16[2,256,1408]{2,1,0:T(8,128)(2,1)} collective-permute-done((bf16[2,256,1408]{2,1,0:T(8,128)(2,1)S(1)}, bf16[2,256,1408]{2,1,0:T(8,128)(2,1)}, u32[]{:S(2)}, u32[]{:S(2)}) %collective-permute-start.1) | collective-permute-done | bytes 1441824 | tf_op jit(solution)/shard_map/ppermute | solution.py:563
  541.3 0.5 slice.9
  541.8 0.5 slice.8
  542.3 1.4 broadcast_in_dim.17
  543.9 1.1 broadcast_in_dim.15
  545.2 1.5 constant_dynamic-update-slice_fusion.2
  546.7 1.5 constant_dynamic-update-slice_fusion.1
  548.2 1.6 constant_dynamic-update-slice_fusion.6
  549.8 1.6 constant_dynamic-update-slice_fusion.5
  551.4 1.5 constant_dynamic-update-slice_fusion
  552.9 2.7 constant_dynamic-update-slice_fusion.4
  555.6 2.5 copy-done.1
  (19 shorter events, 0.4 us)
Async XLA Ops:
  468.4 9.0 %copy-start.2 = (f32[2,256,1408]{2,1,0:T(8,128)S(1)}, f32[2,256,1408]{2,1,0:T(8,128)}, u32[]{:S(2)}) copy-start(f32[2,256,1408]{2,1,0:T(8,128)} %param.16) | copy-start | bytes 8650756
  468.4 9.0 %copy-start.3 = (f32[2,256,1408]{2,1,0:T(8,128)S(1)}, f32[2,256,1408]{2,1,0:T(8,128)}, u32[]{:S(2)}) copy-start(f32[2,256,1408]{2,1,0:T(8,128)} %param.18) | copy-start | bytes 8650756
  468.4 9.9 %copy-start.4 = (f32[2,256,1408]{2,1,0:T(8,128)S(1)}, f32[2,256,1408]{2,1,0:T(8,128)}, u32[]{:S(2)}) copy-start(f32[2,256,1408]{2,1,0:T(8,128)} %param.20) | copy-start | bytes 8650756
  468.4 10.2 %copy-start.5 = (f32[256,1408]{1,0:T(8,128)S(1)}, f32[256,1408]{1,0:T(8,128)}, u32[]{:S(2)}) copy-start(f32[256,1408]{1,0:T(8,128)} %get-tuple-element.28) | copy-start | bytes 4325380
  468.5 10.6 %copy-start.6 = (f32[256,1408]{1,0:T(8,128)S(1)}, f32[256,1408]{1,0:T(8,128)}, u32[]{:S(2)}) copy-start(f32[256,1408]{1,0:T(8,128)} %get-tuple-element.27) | copy-start | bytes 4325380
  476.8 34.5 %collective-permute-start.4 = (bf16[2,352,1024]{2,1,0:T(8,128)(2,1)S(1)}, bf16[2,352,1024]{2,1,0:T(8,128)(2,1)}, u32[]{:S(2)}, u32[]{:S(2)}) collective-permute-start(bf16[2,352,1024]{2,1,0:T(8,128)(2,1)S(1)} %get-tuple-element.31), channel_id=1, source_target_pairs={{0,2},{1,3},{2,0},{3,1},{4,6},{5,7},{6,4},{7,5}} | collective-permute-start | bytes 4325384 | tf_op jit(solution)/shard_map/ppermute | solution.py:563
  483.5 57.8 %collective-permute-start.1 = (bf16[2,256,1408]{2,1,0:T(8,128)(2,1)S(1)}, bf16[2,256,1408]{2,1,0:T(8,128)(2,1)}, u32[]{:S(2)}, u32[]{:S(2)}) collective-permute-start(bf16[2,256,1408]{2,1,0:T(8,128)(2,1)S(1)} %get-tuple-element.35), channel_id=1, source_target_pairs={{0,2},{1,3},{2,0},{3,1},{4,6},{5,7},{6,4},{7,5}} | collective-permute-start | bytes 4325384 | tf_op jit(solution)/shard_map/ppermute | solution.py:563
  484.2 61.0 %collective-permute-start.3 = (bf16[2,352,1024]{2,1,0:T(8,128)(2,1)S(1)}, bf16[2,352,1024]{2,1,0:T(8,128)(2,1)}, u32[]{:S(2)}, u32[]{:S(2)}) collective-permute-start(bf16[2,352,1024]{2,1,0:T(8,128)(2,1)S(1)} %get-tuple-element.31), channel_id=1, source_target_pairs={{0,1},{1,0},{2,3},{3,2},{4,5},{5,4},{6,7},{7,6}} | collective-permute-start | bytes 4325384 | tf_op jit(solution)/shard_map/ppermute | solution.py:564
  484.2 64.0 %collective-permute-start = (bf16[2,256,1408]{2,1,0:T(8,128)(2,1)S(1)}, bf16[2,256,1408]{2,1,0:T(8,128)(2,1)}, u32[]{:S(2)}, u32[]{:S(2)}) collective-permute-start(bf16[2,256,1408]{2,1,0:T(8,128)(2,1)S(1)} %get-tuple-element.35), channel_id=1, source_target_pairs={{0,1},{1,0},{2,3},{3,2},{4,5},{5,4},{6,7},{7,6}} | collective-permute-start | bytes 4325384 | tf_op jit(solution)/shard_map/ppermute | solution.py:564
  511.3 40.1 %collective-permute-start.5 = (bf16[2,352,1024]{2,1,0:T(8,128)(2,1)}, bf16[2,352,1024]{2,1,0:T(8,128)(2,1)}, u32[]{:S(2)}, u32[]{:S(2)}) collective-permute-start(bf16[2,352,1024]{2,1,0:T(8,128)(2,1)} %collective-permute-done.4), channel_id=1, source_target_pairs={{0,1},{1,0},{2,3},{3,2},{4,5},{5,4},{6,7},{7,6}} | collective-permute-start | bytes 4325384 | tf_op jit(solution)/shard_map/ppermute | solution.py:565
  541.3 11.6 %collective-permute-start.2 = (bf16[2,256,1408]{2,1,0:T(8,128)(2,1)}, bf16[2,256,1408]{2,1,0:T(8,128)(2,1)}, u32[]{:S(2)}, u32[]{:S(2)}) collective-permute-start(bf16[2,256,1408]{2,1,0:T(8,128)(2,1)} %collective-permute-done.1), channel_id=1, source_target_pairs={{0,1},{1,0},{2,3},{3,2},{4,5},{5,4},{6,7},{7,6}} | collective-permute-start | bytes 4325384 | tf_op jit(solution)/shard_map/ppermute | solution.py:565
  552.9 2.7 copy-start
  555.6 2.5 copy-start.1
